TPU v7x, 32 devices: a 4x4x1 block of a 4x4x8 slice. The times are simulated.
32 devices in a mesh: layer: 1 (over z), tensor: 32 (over y, x, core).
Axes of the slice: x: 4, y: 4, z: 1, core: 2. Of those that a mesh axis runs over, the one named last changes fastest.
The devices are a block of a 4x4x8 slice.
Arguments:
- gradient: bfloat16 [4096, 8192], P('layer', 'tensor')
- left_stat: float32 [4096, 4096], P(('layer', 'tensor'))
- right_stat: float32 [8192, 8192], P(('layer', 'tensor'))
- left_root: bfloat16 [4096, 4096], P(('layer', 'tensor'))
- right_root: bfloat16 [8192, 8192], P(('layer', 'tensor'))
Outputs:
- output 1: float32 [4096, 4096], P(('layer', 'tensor'))
- output 2: float32 [8192, 8192], P(('layer', 'tensor'))
- output 3: float32 [4096, 8192], P('layer', 'tensor')
All inputs are finite; a program needn't handle non-finite values.
Results may differ from a plain program's by a relative error of at most 0.001.
Values are sent between devices in bfloat16 or wider.
A program may use at most 768 MiB of HBM per device.

v0:
```python
import jax
import jax.numpy as jnp
from jax import lax
from jax.sharding import PartitionSpec as P

EMA_DECAY = 0.9


def solution(mesh):
    row_spec = P(("layer", "tensor"), None)
    col_spec = P("layer", "tensor")

    def local_step(grad_local, left_block, right_block, left_root_block, right_root_block):
        grad_full = lax.all_gather(grad_local, "tensor", axis=1, tiled=True)
        left_part = jnp.einsum("mc,kc->mk", grad_local, grad_local, preferred_element_type=jnp.float32)
        left_sum = lax.psum_scatter(left_part, "tensor", scatter_dimension=0, tiled=True)
        left_new = EMA_DECAY * left_block + (1.0 - EMA_DECAY) * left_sum
        right_prod = jnp.einsum("mc,mn->cn", grad_local, grad_full, preferred_element_type=jnp.float32)
        right_new = EMA_DECAY * right_block + (1.0 - EMA_DECAY) * right_prod
        precond = jnp.einsum("mn,cn->mc", grad_full, right_root_block, preferred_element_type=jnp.float32).astype(jnp.bfloat16)
        left_root_full = lax.all_gather(left_root_block, "tensor", axis=0, tiled=True)
        direction = jnp.dot(left_root_full, precond, preferred_element_type=jnp.float32)
        return left_new, right_new, direction

    return jax.shard_map(local_step, mesh=mesh, in_specs=(col_spec, row_spec, row_spec, row_spec, row_spec), out_specs=(row_spec, row_spec, col_spec), check_vma=False)
```

profile of v0, /device:TPU:97, one launch (start us, length us, event | category | flops | bytes accessed | tf_op | source)
XLA Modules:
  0.0 706.4 jit_solution(16176768652187271183)
XLA Ops:
  7.2 0.1 reduce-scatter.2.cloned.1.call-start
  7.2 26.1 %fusion.1 = f32[4096,4096]{1,0:T(8,128)} fusion(bf16[4096,256]{1,0:T(8,128)(2,1)} %param.5), kind=kOutput, calls=%fused_computation.5 | convolution fusion | flops 8589934592 | bytes 69206016 | tf_op jit(solution)/shard_map/mc,kc->mk/dot_general | solution.py:15
  33.4 0.1 reduce-scatter.2.cloned.1.call-update
  33.4 0.0 copy-start.1
  33.4 0.1 all-gather.3.cloned.1.call-start
  33.5 0.7 all-gather.3.cloned.1.call-update
  34.2 0.1 all-gather.5.cloned.1.call-start
  34.3 0.7 all-gather.5.cloned.1.call-update
  35.0 286.7 %reduce-scatter.2.cloned.1.call-done = f32[128,4096]{1,0:T(8,128)} async-done(((f32[4096,4096]{1,0:T(8,128)}), f32[128,4096]{1,0:T(8,128)}) %reduce-scatter.2.cloned.1.call-update) | async-done | bytes 2097168 | tf_op jit(solution)/shard_map/reduce_scatter | solution.py:16
  321.8 0.0 copy-done.1
  321.8 3.2 multiply_add_fusion
  325.0 209.3 %all-gather.3.cloned.1.call-done = bf16[4096,8192]{1,0:T(8,128)(2,1)} async-done(((bf16[4096,256]{1,0:T(8,128)(2,1)}), bf16[4096,8192]{1,0:T(8,128)(2,1)}) %all-gather.3.cloned.1.call-update) | async-done | bytes 67108880 | tf_op jit(solution)/shard_map/all_gather | solution.py:14
  534.4 26.8 %fusion.27 = bf16[4096,256]{1,0:T(8,128)(2,1)S(1)} fusion(bf16[256,8192]{1,0:T(8,128)(2,1)} %param.9, bf16[4096,8192]{1,0:T(8,128)(2,1)} %all-gather.3.cloned.1.call-done), kind=kOutput, calls=%bitcast_fusion.1.clone.1 | convolution fusion | flops 17180917760 | bytes 73400320 | tf_op jit(solution)/shard_map/mn,cn->mc/dot_general | solution.py:20
  561.2 84.4 %all-gather.5.cloned.1.call-done = bf16[4096,4096]{1,0:T(8,128)(2,1)} async-done(((bf16[128,4096]{1,0:T(8,128)(2,1)}), bf16[4096,4096]{1,0:T(8,128)(2,1)}) %all-gather.5.cloned.1.call-update) | async-done | bytes 33554448 | tf_op jit(solution)/shard_map/all_gather | solution.py:21
  645.6 16.2 %convolution_bitcast_fusion = f32[4096,256]{0,1:T(8,128)} fusion(bf16[4096,4096]{1,0:T(8,128)(2,1)} %all-gather.5.cloned.1.call-done, bf16[4096,256]{1,0:T(8,128)(2,1)S(1)} %fusion.27), kind=kOutput, calls=%fused_computation.2 | convolution fusion | flops 8589934592 | bytes 39845888 | tf_op jit(solution)/shard_map/dot_general | solution.py:22
  661.8 0.0 copy-start
  661.8 5.7 copy.8
  667.6 0.0 copy-done
  667.6 32.2 %fusion = f32[256,8192]{1,0:T(8,128)} fusion(bf16[4096,256]{1,0:T(8,128)(2,1)S(1)} %copy-done, bf16[4096,8192]{1,0:T(8,128)(2,1)} %all-gather.3.cloned.1.call-done, f32[256,8192]{1,0:T(8,128)} %param.7), kind=kOutput, calls=%fused_computation.1 | convolution fusion | flops 17186160640 | bytes 85983232 | tf_op jit(solution)/shard_map/mc,mn->cn/dot_general | solution.py:18
Async XLA Ops:
  7.2 314.6 %reduce-scatter.2.cloned.1.call-start = ((), (), s32[]{:S(2)}) async-start(), calls=%async_computation.1 | async-start | bytes 69206016 | tf_op jit(solution)/shard_map/reduce_scatter | solution.py:16
  33.4 288.4 %copy-start.1 = (f32[128,4096]{1,0:T(8,128)S(1)}, f32[128,4096]{1,0:T(8,128)}, u32[]{:S(2)}) copy-start(f32[128,4096]{1,0:T(8,128)} %param.6) | copy-start | bytes 6291460
  33.4 500.9 %all-gather.3.cloned.1.call-start = ((), (), s32[]{:S(2)}) async-start(), calls=%async_computation.2 | async-start | bytes 69206016 | tf_op jit(solution)/shard_map/all_gather | solution.py:14
  34.2 611.3 %all-gather.5.cloned.1.call-start = ((), (), s32[]{:S(2)}) async-start(), calls=%async_computation.3 | async-start | bytes 34603008 | tf_op jit(solution)/shard_map/all_gather | solution.py:21
  661.8 5.7 copy-start
Sparse Core Ops, SparseCore 0:
  33.5 288.1 reduce-scatter.1
  323.8 210.5 all-gather.2
  536.4 109.0 all-gather.4
where the time goes:
time: 707 us; the launch traced here: 706 us
  waiting for transfers between devices  582 us (82%)
  matrix products  101 us (14%)
  between operations  13.8 us (2%)
    reduce_scatter x1, waiting for transfers between devices, local_step(): lax.psum_scatter(left_part, 'tensor', scatter_dimension=0, tiled=True)  287 us
    all_gather x1, waiting for transfers between devices, local_step(): grad_full = lax.all_gather(grad_local, 'tensor', axis=1, tiled=True)  209 us
    all_gather x1, waiting for transfers between devices, local_step(): lax.all_gather(left_root_block, 'tensor', axis=0, tiled=True)  84.4 us
    dot_general x1, matrix products, local_step(): jnp.einsum('mc,mn->cn', grad_local, grad_full, preferred_element_type=jnp...  32.2 us
    dot_general x1, matrix products, local_step(): jnp.einsum('mn,cn->mc', grad_full, right_root_block, preferred_element_ty...  26.8 us
    dot_general x1, matrix products, local_step(): jnp.einsum('mc,kc->mk', grad_local, grad_local, preferred_element_type=jn...  26.1 us
    dot_general x1, matrix products, local_step(): jnp.dot(left_root_full, precond, preferred_element_type=jnp.float32)  16.2 us
  transfers between devices with their start and end apart: 3, of which 3 were waited for; matrix products, arithmetic and copies ran while one was open for 4% of the time, Pallas kernels for 0%

commit v1 on v0

v1 whole, which is shorter than its diff:
```python
import jax
import jax.numpy as jnp
from jax import lax
from jax.sharding import PartitionSpec as P

EMA_DECAY = 0.9


def solution(mesh):
    row_spec = P(("layer", "tensor"), None)
    col_spec = P("layer", "tensor")

    def local_step(grad_local, left_block, right_block, left_root_block, right_root_block):
        rows = left_block.shape[0]
        grad_full = lax.all_gather(grad_local, "tensor", axis=1, tiled=True)
        grad_full, left_root_block = lax.optimization_barrier((grad_full, left_root_block))
        left_root_full = lax.all_gather(left_root_block, "tensor", axis=0, tiled=True)
        precond = jnp.einsum("mn,cn->mc", grad_full, right_root_block, preferred_element_type=jnp.float32).astype(jnp.bfloat16)
        right_prod = jnp.einsum("mc,mn->cn", grad_local, grad_full, preferred_element_type=jnp.float32)
        right_new = EMA_DECAY * right_block + (1.0 - EMA_DECAY) * right_prod
        grad_rows = lax.dynamic_slice_in_dim(grad_full, lax.axis_index("tensor") * rows, rows, axis=0)
        left_prod = jnp.einsum("rn,mn->rm", grad_rows, grad_full, preferred_element_type=jnp.float32)
        left_new = EMA_DECAY * left_block + (1.0 - EMA_DECAY) * left_prod
        direction = jnp.dot(left_root_full, precond, preferred_element_type=jnp.float32)
        return left_new, right_new, direction

    return jax.shard_map(local_step, mesh=mesh, in_specs=(col_spec, row_spec, row_spec, row_spec, row_spec), out_specs=(row_spec, row_spec, col_spec), check_vma=False)
```

time: 707 us -> 360 us (0.51)
  waiting for transfers between devices: 582 us -> 220 us
  local copies, waits for them, and re-layouts: 5.75 us -> 18.2 us
    reduce_scatter x1 -> x0, waiting for transfers between devices: 287 us -> none  [local_step(): lax.psum_scatter(left_part, 'tensor', scatter_dimension=0, tiled=True)]
    all_gather x1, waiting for transfers between devices: 84.4 us -> 3.19 us  [local_step(): lax.all_gather(left_root_block, 'tensor', axis=0, tiled=True)]
    unnamed x5 -> x6, local copies, waits for them, and re-layouts: 5.75 us -> 18.2 us
    all_gather x1, waiting for transfers between devices: 209 us -> 217 us  [local_step(): grad_full = lax.all_gather(grad_local, 'tensor', axis=1, tiled=True)]
  transfers between devices with their start and end apart: 3 -> 2, of which waited for: 3 -> 2; matrix products, arithmetic and copies ran while one was open for 4% -> 30% of each run, Pallas kernels for 0% -> 0%
where the time goes in v1:
time: 360 us
  waiting for transfers between devices  220 us (61%)
  matrix products  107 us (30%)
  local copies, waits for them, and re-layouts  18.2 us (5%)
  between operations  14.1 us (4%)
    all_gather x1, waiting for transfers between devices, local_step(): grad_full = lax.all_gather(grad_local, 'tensor', axis=1, tiled=True)  217 us
    dot_general x1, matrix products, local_step(): jnp.einsum('mc,mn->cn', grad_local, grad_full, preferred_element_type=jnp...  33.1 us
    dot_general x1, matrix products, local_step(): jnp.einsum('rn,mn->rm', grad_rows, grad_full, preferred_element_type=jnp....  29.8 us
    dot_general x1, matrix products, local_step(): jnp.einsum('mn,cn->mc', grad_full, right_root_block, preferred_element_ty...  26.8 us
    unnamed x6, local copies, waits for them, and re-layouts  18.2 us
    dot_general x1, matrix products, local_step(): jnp.dot(left_root_full, precond, preferred_element_type=jnp.float32)  17.1 us
  transfers between devices with their start and end apart: 2, of which 2 were waited for; matrix products, arithmetic and copies ran while one was open for 30% of the time, Pallas kernels for 0%

profile of v1, /device:TPU:97, one launch (start us, length us, event | category | flops | bytes accessed | tf_op | source)
XLA Modules:
  0.0 359.7 jit_solution(10823795718367896129)
XLA Ops:
  7.2 0.1 all-gather.3.cloned.1.call-start
  7.2 0.7 all-gather.3.cloned.1.call-update
  8.0 0.1 all-gather.5.cloned.1.call-start
  8.0 216.5 %all-gather.3.cloned.1.call-done = bf16[4096,8192]{1,0:T(8,128)(2,1)} async-done(((bf16[4096,256]{1,0:T(8,128)(2,1)}), bf16[4096,8192]{1,0:T(8,128)(2,1)}) %all-gather.3.cloned.1.call-update) | async-done | bytes 67108880 | tf_op jit(solution)/shard_map/all_gather | solution.py:15
  224.6 0.1 all-gather.5.cloned.1.call-update
  224.6 0.0 copy-start.1
  224.6 9.1 %copy.8 = f32[256,8192]{0,1:T(8,128)} copy(f32[256,8192]{1,0:T(8,128)} %param.7) | data formatting | bytes 16777216 | tf_op args[2]
  233.8 0.0 copy-done.1
  233.8 33.1 %fusion.1 = f32[256,8192]{0,1:T(8,128)} fusion(bf16[4096,8192]{1,0:T(8,128)(2,1)} %all-gather.3.cloned.1.call-done, bf16[4096,256]{1,0:T(8,128)(2,1)S(1)} %copy-done.1, f32[256,8192]{0,1:T(8,128)} %copy.8), kind=kOutput, calls=%fused_computation.2 | convolution fusion | flops 17186160640 | bytes 85983232 | tf_op jit(solution)/shard_map/mc,mn->cn/dot_general | solution.py:19
  266.9 0.0 copy-start
  266.9 9.0 %copy.9 = f32[256,8192]{1,0:T(8,128)} copy(f32[256,8192]{0,1:T(8,128)} %fusion.1) | data formatting | bytes 16777216
  276.0 0.0 copy-done
  276.0 29.8 %fusion.2 = f32[128,4096]{1,0:T(8,128)} fusion(bf16[4096,8192]{1,0:T(8,128)(2,1)} %all-gather.3.cloned.1.call-done, s32[]{:T(128)S(6)} %select_n.3, f32[128,4096]{1,0:T(8,128)S(1)} %copy-done), kind=kOutput, calls=%fused_computation.5 | convolution fusion | flops 8591507456 | bytes 73400320 | tf_op jit(solution)/shard_map/rn,mn->rm/dot_general | solution.py:22
  305.7 26.8 %fusion.30 = bf16[4096,256]{1,0:T(8,128)(2,1)S(1)} fusion(bf16[256,8192]{1,0:T(8,128)(2,1)} %param.9, bf16[4096,8192]{1,0:T(8,128)(2,1)} %all-gather.3.cloned.1.call-done), kind=kOutput, calls=%bitcast_fusion.6.clone.1 | convolution fusion | flops 17180917760 | bytes 73400320 | tf_op jit(solution)/shard_map/mn,cn->mc/dot_general | solution.py:18
  332.6 3.2 all-gather.5.cloned.1.call-done
  335.8 17.1 %fusion.5 = f32[4096,256]{1,0:T(8,128)} fusion(bf16[4096,4096]{1,0:T(8,128)(2,1)} %all-gather.5.cloned.1.call-done, bf16[4096,256]{1,0:T(8,128)(2,1)S(1)} %fusion.30), kind=kOutput, calls=%fused_computation.8 | convolution fusion | flops 8589934592 | bytes 39845888 | tf_op jit(solution)/shard_map/dot_general | solution.py:24
Async XLA Ops:
  7.2 217.4 %all-gather.3.cloned.1.call-start = ((), (), s32[]{:S(2)}) async-start(), calls=%async_computation | async-start | bytes 69206016 | tf_op jit(solution)/shard_map/all_gather | solution.py:15
  8.0 327.8 %all-gather.5.cloned.1.call-start = ((), (), s32[]{:S(2)}) async-start(), calls=%async_computation.1 | async-start | bytes 34603008 | tf_op jit(solution)/shard_map/all_gather | solution.py:17
  224.6 9.2 %copy-start.1 = (bf16[4096,256]{1,0:T(8,128)(2,1)S(1)}, bf16[4096,256]{1,0:T(8,128)(2,1)}, u32[]{:S(2)}) copy-start(bf16[4096,256]{1,0:T(8,128)(2,1)} %param.5) | copy-start | bytes 6291460
  266.9 9.0 %copy-start = (f32[128,4096]{1,0:T(8,128)S(1)}, f32[128,4096]{1,0:T(8,128)}, u32[]{:S(2)}) copy-start(f32[128,4096]{1,0:T(8,128)} %param.6) | copy-start | bytes 6291460
Sparse Core Ops, SparseCore 0:
  10.0 214.5 all-gather.2
  226.6 109.0 all-gather.4

commit v2 on v0

v2 whole, which is shorter than its diff:
```python
import functools
import math

import jax
import jax.numpy as jnp
from jax import lax
from jax.experimental import pallas as pl
from jax.experimental.pallas import tpu as pltpu
from jax.sharding import PartitionSpec as P

EMA_DECAY = 0.9
CORES = 2
MESH = pl.DeviceIdType.MESH

ORDER = [(0, 0), (3, 0), (1, 0), (0, 3), (0, 1), (2, 0), (0, 2), (3, 3), (1, 1), (1, 3), (3, 1), (2, 3), (2, 1), (3, 2), (1, 2), (2, 2)]
UP = [
    ((0, 3), 0, True), ((0, 3), 1, False), ((3, 3), 0, True), ((1, 3), 1, False), ((0, 2), 0, False), ((3, 3), 1, False),
    ((1, 3), 0, True), ((2, 3), 0, True), ((2, 3), 1, False), ((3, 2), 0, False), ((1, 2), 0, False), ((2, 2), 0, False),
]
DOWN = [
    ((0, 1), 1, True), ((0, 1), 0, False), ((1, 1), 1, True), ((3, 1), 0, False), ((0, 2), 1, False), ((1, 1), 0, False),
    ((3, 1), 1, True), ((2, 1), 1, True), ((2, 1), 0, False), ((1, 2), 1, False), ((3, 2), 1, False), ((2, 2), 1, False),
]
ROUNDS = len(UP)
FIRST_UP = [((3, 0), 0, True), ((3, 0), 1, False), ((2, 0), 0, False)]
FIRST_DOWN = [((1, 0), 1, True), ((1, 0), 0, False), ((2, 0), 1, False)]
GRAD_ROUND_STEP = [2, 2, 8, 10, 12, 14, 17, 20, 22, 24, 26, 30]
ROOT_ROUND_STEP = [2, 2, 8, 10, 12, 14, 17, 20, 22, 24, 26, 30]
LATE = (2, 12, 14, 22, 26, 30)


def packed(values):
    return [sum(v << (2 * i) for i, v in enumerate(values[j:j + 8])) for j in (0, 8)]


FIRST_CODE = packed([o[0] for o in ORDER])
SECOND_CODE = packed([o[1] for o in ORDER])


def lookup(code, e):
    word = code[0] + (e // 8) * (code[1] - code[0])
    return lax.shift_right_logical(word, 2 * (e % 8)) & 3


def kernel(n, side, g_ref, l_ref, r_ref, lr_ref, rr_ref, lo_out, ro_out, do_out, gfull, lfull,
           lo_ref, ro_ref, do_ref, rr, gt, acc, gbuf, lbuf, rhs, xbf, g_recv, l_recv, g_send, l_send, load_sem, init_sem, out_sem):
    _, half_rows, cols = g_ref.shape
    rows = 2 * half_rows
    lrows = l_ref.shape[0]
    tile = min(1024, half_rows)

    me = lax.axis_index("tensor")
    c = me % CORES
    chip = me // CORES
    x, y = chip % side, chip // side
    f = x + c * (y - x)
    s = y + c * (x - y)
    fstep = CORES + c * CORES * (side - 1)
    sstep = CORES * side - c * CORES * (side - 1)
    twin = me + 1 - 2 * c

    def index(df, ds):
        return ((f + df) % side) * fstep + ((s + ds) % side) * sstep + c

    def twin_index(df, ds):
        return ((s + df) % side) * sstep + ((f + ds) % side) * fstep + 1 - c

    peers = {"f+": index(1, 0), "f-": index(3, 0), "s+": index(0, 1), "s-": index(0, 3), "twin": twin}
    slot_of = {name: i for i, name in enumerate(peers)}

    class Gather:
        def __init__(self, own, full, recv, send):
            self.own, self.full, self.recv, self.send_sem = own, full, recv, send
            self.count = {name: 0 for name in peers}

        def copy(self, name, b, half, own=False):
            src = self.own.at[half] if own else self.full.at[2 * b + half]
            return pltpu.make_async_remote_copy(
                src_ref=src, dst_ref=self.full.at[2 * b + half], send_sem=self.send_sem.at[slot_of[name]],
                recv_sem=self.recv.at[2 * b + half], device_id={"tensor": peers[name]}, device_id_type=MESH)

        def send(self, name, b, half, own=False):
            self.count[name] += 1
            self.copy(name, b, half, own).start()

        def wait(self, b, half):
            self.copy("twin", b, half).wait_recv()

        def start(self):
            for half in (0, 1):
                for name in ("f+", "s+"):
                    self.send(name, me, half, own=True)
                for name in ("f-", "s-"):
                    self.send(name, me, 1 - half, own=True)
            for half in (0, 1):
                self.send("twin", me, half, own=True)

        def round(self, r):
            if r < len(FIRST_UP):
                (ou, hu, on), (od, hd, _) = FIRST_UP[r], FIRST_DOWN[r]
                bu, bd = index(*ou), index(*od)
                self.wait(bu, hu)
                if on:
                    self.send("f+", bu, hu)
                self.wait(bd, hd)
                if on:
                    self.send("f-", bd, hd)
                self.send("s+", bu, hu)
                self.send("s-", bd, hd)
                self.send("s+", bd, hd)
                self.send("s-", bu, hu)
                self.send("twin", bu, hu)
                self.send("twin", bd, hd)
            (ou, hu, on), (od, hd, _) = UP[r], DOWN[r]
            bu, bd = index(*ou), index(*od)
            self.wait(bu, hu)
            if on:
                self.send("s+", bu, hu)
            self.send("twin", bu, hu)
            self.wait(bd, hd)
            if on:
                self.send("s-", bd, hd)
            self.send("twin", bd, hd)

        def drain(self):
            for name, count in self.count.items():
                whole = self.full.at[pl.ds(0, count)]
                pltpu.make_async_copy(whole, whole, self.send_sem.at[slot_of[name]]).wait()

    grad = Gather(g_ref, gfull, g_recv, g_send)
    root = Gather(lr_ref, lfull, l_recv, l_send)

    def block_of(k):
        e, other = k // 2, k % 2
        df, ds = lookup(FIRST_CODE, e), lookup(SECOND_CODE, e)
        mine = index(df, ds)
        return mine + other * (twin_index(df, ds) - mine)

    def load(gather, buf, k, sem):
        b = block_of(k)
        return pltpu.make_async_copy(gather.full.at[pl.ds(2 * b, 2)], buf.at[k % 2], sem.at[k % 2])

    def start_load(gather, buf, k, sem):
        @pl.when(k % 2 == 1)
        def _():
            b = block_of(k)
            gather.wait(b, 0)
            gather.wait(b, 1)
        load(gather, buf, k, sem).start()

    def is_late(k):
        late = k == LATE[0]
        for v in LATE[1:]:
            late = late | (k == v)
        return late

    def steps(gather, buf, sem, round_step, extra, work):
        def step(k, carry):
            for r in range(ROUNDS):
                @pl.when(k == round_step[r])
                def _():
                    gather.round(r)
            for at, fn in extra:
                pl.when(k == at)(fn)

            @pl.when(is_late(k))
            def _():
                start_load(gather, buf, k, sem)

            @pl.when((k + 1 < n) & jnp.logical_not(is_late(k + 1)))
            def _():
                start_load(gather, buf, k + 1, sem)
            load(gather, buf, k, sem).wait()
            work(k, k % 2, block_of(k))
            return carry
        lax.fori_loop(0, n, step, 0)

    first = [
        pltpu.make_async_copy(rr_ref, rr, init_sem.at[0]),
        pltpu.make_async_copy(r_ref, ro_ref, init_sem.at[1]),
        pltpu.make_async_copy(l_ref, lo_ref, init_sem.at[2]),
    ]
    own_load = pltpu.make_async_copy(g_ref, gbuf.at[0], load_sem.at[0])
    own_load.start()

    barrier = pltpu.get_barrier_semaphore()
    for peer in peers.values():
        pl.semaphore_signal(barrier, inc=1, device_id={"tensor": peer}, device_id_type=MESH)
    pl.semaphore_wait(barrier, len(peers))
    grad.start()
    for copy in first:
        copy.start()

    acc[...] = jnp.zeros_like(acc)
    own_load.wait()
    for h in (0, 1):
        gt[:, h * half_rows:(h + 1) * half_rows] = gbuf[0, h].T
    for copy in first:
        copy.wait()
    own_load.start()

    per_half = half_rows // tile

    def grad_work(k, slot, b):
        at = pl.multiple_of(b * cols, cols)
        rhs[:cols] = rr[:, pl.ds(at, cols)]
        rhs[cols:] = gbuf[slot, me // (n // 2), pl.ds(pl.multiple_of((me % (n // 2)) * lrows, lrows), lrows), :]

        def rows_step(t, carry):
            left = gbuf[slot, t // per_half, pl.ds(pl.multiple_of((t % per_half) * tile, tile), tile), :]
            out = pl.ds(pl.multiple_of(t * tile, tile), tile)
            acc[out, :] += lax.dot_general(left, rhs[...], (((1,), (1,)), ((), ())), preferred_element_type=jnp.float32)
            return carry
        lax.fori_loop(0, 2 * per_half, rows_step, 0)
        prod = jnp.dot(gt[:, :half_rows], gbuf[slot, 0], preferred_element_type=jnp.float32)
        prod += jnp.dot(gt[:, half_rows:], gbuf[slot, 1], preferred_element_type=jnp.float32)
        ro_ref[:, pl.ds(at, cols)] = EMA_DECAY * ro_ref[:, pl.ds(at, cols)] + (1.0 - EMA_DECAY) * prod
        pltpu.make_async_copy(ro_ref.at[:, pl.ds(at, cols)], ro_out.at[:, pl.ds(at, cols)], out_sem.at[0]).start()

    steps(grad, gbuf, load_sem, GRAD_ROUND_STEP, [(GRAD_ROUND_STEP[-2], root.start)], grad_work)

    pltpu.make_async_copy(lr_ref, lbuf.at[0], load_sem.at[0]).start()
    xbf[...] = acc[:, :cols].astype(jnp.bfloat16)

    def left_step(t, carry):
        at = pl.ds(pl.multiple_of(t * lrows, lrows), lrows)
        lo_ref[:, at] = EMA_DECAY * lo_ref[:, at] + (1.0 - EMA_DECAY) * acc[at, cols:].T
        return carry
    lax.fori_loop(0, rows // lrows, left_step, 0)
    left_store = pltpu.make_async_copy(lo_ref, lo_out, out_sem.at[1])
    left_store.start()

    def root_work(k, slot, b):
        left = lbuf[slot].reshape(lrows, rows)
        at = pl.ds(pl.multiple_of(b * lrows, lrows), lrows)
        do_ref[at, :] = jnp.dot(left, xbf[...], preferred_element_type=jnp.float32)
        pltpu.make_async_copy(do_ref.at[at], do_out.at[at], out_sem.at[2]).start()

    steps(root, lbuf, load_sem, ROOT_ROUND_STEP, [], root_work)
    grad.drain()
    root.drain()
    pltpu.make_async_copy(ro_ref, ro_out, out_sem.at[0]).wait()
    left_store.wait()
    pltpu.make_async_copy(do_ref, do_out, out_sem.at[2]).wait()


def solution(mesh):
    row_spec = P(("layer", "tensor"), None)
    col_spec = P("layer", "tensor")
    n = mesh.shape["tensor"]
    side = math.isqrt(n // CORES)

    def local_step(g, l, r, lr, rr):
        rows, cols = g.shape
        lrows = l.shape[0]
        hbm = pl.BlockSpec(memory_space=pltpu.HBM)
        left_new, right_new, direction, _, _ = pl.pallas_call(
            functools.partial(kernel, n, side),
            name="shampoo",
            out_shape=[
                jax.ShapeDtypeStruct(l.shape, jnp.float32),
                jax.ShapeDtypeStruct(r.shape, jnp.float32),
                jax.ShapeDtypeStruct(g.shape, jnp.float32),
                jax.ShapeDtypeStruct((2 * n, rows // 2, cols), jnp.bfloat16),
                jax.ShapeDtypeStruct((2 * n, lrows // 2, rows), jnp.bfloat16),
            ],
            in_specs=[hbm] * 5,
            out_specs=[hbm] * 5,
            scratch_shapes=[
                pltpu.VMEM(l.shape, jnp.float32),
                pltpu.VMEM(r.shape, jnp.float32),
                pltpu.VMEM(g.shape, jnp.float32),
                pltpu.VMEM(rr.shape, jnp.bfloat16),
                pltpu.VMEM((cols, rows), jnp.bfloat16),
                pltpu.VMEM((rows, cols + lrows), jnp.float32),
                pltpu.VMEM((2, 2, rows // 2, cols), jnp.bfloat16),
                pltpu.VMEM((2, 2, lrows // 2, rows), jnp.bfloat16),
                pltpu.VMEM((cols + lrows, cols), jnp.bfloat16),
                pltpu.VMEM((rows, cols), jnp.bfloat16),
                pltpu.SemaphoreType.DMA((2 * n,)),
                pltpu.SemaphoreType.DMA((2 * n,)),
                pltpu.SemaphoreType.DMA((5,)),
                pltpu.SemaphoreType.DMA((5,)),
                pltpu.SemaphoreType.DMA((2,)),
                pltpu.SemaphoreType.DMA((3,)),
                pltpu.SemaphoreType.DMA((3,)),
            ],
            compiler_params=pltpu.CompilerParams(collective_id=0, has_side_effects=True, vmem_limit_bytes=62 * 2**20),
            cost_estimate=pl.CostEstimate(flops=2 * rows * cols * (2 * n * cols + 2 * rows), bytes_accessed=2 * n * rows * cols * 3, transcendentals=0),
        )(g.reshape(2, rows // 2, cols), l, r, lr.reshape(2, lrows // 2, rows), rr)
        return left_new, right_new, direction

    return jax.shard_map(local_step, mesh=mesh, in_specs=(col_spec, row_spec, row_spec, row_spec, row_spec), out_specs=(row_spec, row_spec, col_spec), check_vma=False)
```

time: 707 us -> 286 us (0.40)
  waiting for transfers between devices: 582 us -> 0 us
  Pallas kernels: 0 us -> 271 us
  matrix products: 101 us -> 0 us
  between operations: 13.8 us -> 0.64 us
  local copies, waits for them, and re-layouts: 5.75 us -> 13 us
    all_gather x2 -> x0, waiting for transfers between devices: 294 us -> none  [the longest x1 209 us: local_step(): grad_full = lax.all_gather(grad_local, 'tensor', axis=1, tiled=True)]
    reduce_scatter x1 -> x0, waiting for transfers between devices: 287 us -> none  [local_step(): lax.psum_scatter(left_part, 'tensor', scatter_dimension=0, tiled=True)]
    pallas_call x0 -> x1, Pallas kernels: none -> 271 us  [local_step(): pl.pallas_call(functools.partial(kernel, n, side), name='shampoo', out_sh...]
    dot_general x4 -> x0, matrix products: 101 us -> none  [the longest x1 32.2 us: local_step(): jnp.einsum('mc,mn->cn', grad_local, grad_full, preferred_element_type=jnp...]
    unnamed x5, local copies, waits for them, and re-layouts: 5.75 us -> 13 us
  transfers between devices with their start and end apart: 3 -> 0, of which waited for: 3 -> 0; matrix products, arithmetic and copies ran while one was open for 4% -> 0% of each run, Pallas kernels for 0% -> 0%
where the time goes in v2:
time: 286 us; the launch traced here: 285 us
  Pallas kernels  271 us (95%)
  local copies, waits for them, and re-layouts  13 us (5%)
    pallas_call x1, Pallas kernels, local_step(): pl.pallas_call(functools.partial(kernel, n, side), name='shampoo', out_sh...  271 us
    unnamed x5, local copies, waits for them, and re-layouts  13 us

profile of v2, /device:TPU:97, one launch (start us, length us, event | category | flops | bytes accessed | tf_op | source)
XLA Modules:
  0.0 284.8 jit_solution(2749555294413555047)
XLA Ops:
  0.6 271.2 %shampoo.1 = (f32[128,4096]{1,0:T(8,128)}, f32[256,8192]{1,0:T(8,128)}, f32[4096,256]{1,0:T(8,128)}, bf16[64,2048,256]{2,1,0:T(8,128)(2,1)}, bf16[64,64,4096]{2,1,0:T(8,128)(2,1)}) custom-call(bf16[2,2048,256]{2,1,0:T(8,128)(2,1)} %bitcast.2, f32[128,4096]{1,0:T(8,128)} %l_ref.1, f32[256,8192]{1,0:T(8,128)} %r_ref.1, bf16[2,64,4096]{2,1,0:T(8,128)(2,1)} %bitcast.3, ...), custom_call_target="tpu_custom_call" | custom-call | flops 51539607552 | bytes 201326592 | tf_op jit(solution)/shard_map/shampoo/pallas_call | solution.py:257
  271.8 3.1 %copy.11 = f32[128,4096]{1,0:T(8,128)} copy(f32[128,4096]{1,0:T(8,128)} %get-tuple-element.12) | data formatting | bytes 4194304
  275.0 0.0 copy-start
  275.0 7.8 %copy.12 = f32[256,8192]{1,0:T(8,128)} copy(f32[256,8192]{1,0:T(8,128)} %get-tuple-element.13) | data formatting | bytes 16777216
  282.8 0.0 copy-done
  282.8 2.0 copy.13
Async XLA Ops:
  275.0 7.8 %copy-start = (f32[4096,256]{1,0:T(8,128)S(1)}, f32[4096,256]{1,0:T(8,128)}, u32[]{:S(2)}) copy-start(f32[4096,256]{1,0:T(8,128)} %get-tuple-element.14) | copy-start | bytes 12582916

commit v3 on v2

--- a/solution.py
+++ b/solution.py
@@ -25,7 +25,7 @@
 FIRST_UP = [((3, 0), 0, True), ((3, 0), 1, False), ((2, 0), 0, False)]
 FIRST_DOWN = [((1, 0), 1, True), ((1, 0), 0, False), ((2, 0), 1, False)]
 GRAD_ROUND_STEP = [2, 2, 8, 10, 12, 14, 17, 20, 22, 24, 26, 30]
-ROOT_ROUND_STEP = [2, 2, 8, 10, 12, 14, 17, 20, 22, 24, 26, 30]
+ROOT_START_STEP = 29
 LATE = (2, 12, 14, 22, 26, 30)
 
 
@@ -42,8 +42,14 @@
     return lax.shift_right_logical(word, 2 * (e % 8)) & 3
 
 
-def kernel(n, side, g_ref, l_ref, r_ref, lr_ref, rr_ref, lo_out, ro_out, do_out, gfull, lfull,
-           lo_ref, ro_ref, do_ref, rr, gt, acc, gbuf, lbuf, rhs, xbf, g_recv, l_recv, g_send, l_send, load_sem, init_sem, out_sem):
+ROOT_ORDER = [(0, 0), (3, 0), (1, 0), (0, 1), (2, 0), (3, 1), (1, 1), (2, 1)]
+ROOT_Y = sum(o[0] << (2 * i) for i, o in enumerate(ROOT_ORDER))
+ROOT_X = sum(o[1] << (2 * i) for i, o in enumerate(ROOT_ORDER))
+
+
+def kernel(n, side, g_ref, l_ref, r_ref, lr_ref, rr_ref, lo_ref, ro_ref, do_ref, gfull,
+           rr, gt, acc, gbuf, rhs, xx, lroot, relay, lent,
+           g_recv, g_send, load_sem, init_sem, l_recv, relay_recv, x_recv, d_recv, l_send, x_send, d_send):
     _, half_rows, cols = g_ref.shape
     rows = 2 * half_rows
     lrows = l_ref.shape[0]
@@ -128,7 +134,6 @@
                 pltpu.make_async_copy(whole, whole, self.send_sem.at[slot_of[name]]).wait()
 
     grad = Gather(g_ref, gfull, g_recv, g_send)
-    root = Gather(lr_ref, lfull, l_recv, l_send)
 
     def block_of(k):
         e, other = k // 2, k % 2
@@ -179,6 +184,7 @@
         pltpu.make_async_copy(rr_ref, rr, init_sem.at[0]),
         pltpu.make_async_copy(r_ref, ro_ref, init_sem.at[1]),
         pltpu.make_async_copy(l_ref, lo_ref, init_sem.at[2]),
+        pltpu.make_async_copy(lr_ref, lroot.at[pl.ds(2 * ((y * (side // 2) + x // 2) * CORES + c), 2)], init_sem.at[3]),
     ]
     own_load = pltpu.make_async_copy(g_ref, gbuf.at[0], load_sem.at[0])
     own_load.start()
@@ -215,33 +221,187 @@
         prod = jnp.dot(gt[:, :half_rows], gbuf[slot, 0], preferred_element_type=jnp.float32)
         prod += jnp.dot(gt[:, half_rows:], gbuf[slot, 1], preferred_element_type=jnp.float32)
         ro_ref[:, pl.ds(at, cols)] = EMA_DECAY * ro_ref[:, pl.ds(at, cols)] + (1.0 - EMA_DECAY) * prod
-        pltpu.make_async_copy(ro_ref.at[:, pl.ds(at, cols)], ro_out.at[:, pl.ds(at, cols)], out_sem.at[0]).start()
-
-    steps(grad, gbuf, load_sem, GRAD_ROUND_STEP, [(GRAD_ROUND_STEP[-2], root.start)], grad_work)
-
-    pltpu.make_async_copy(lr_ref, lbuf.at[0], load_sem.at[0]).start()
-    xbf[...] = acc[:, :cols].astype(jnp.bfloat16)
+
+
+    dx = 1 - 2 * c
+    helper = (y * side + (x + dx + side) % side) * CORES + c
+    client = (y * side + (x - dx + side) % side) * CORES + c
+    up = (((y + 1) % side) * side + x) * CORES + c
+    down = (((y + side - 1) % side) * side + x) * CORES + c
+    half_count = lroot.shape[0]
+
+    def root_block(dy, q, p=0):
+        oy, ox = (y + dy) % side, (x + 2 * q) % side
+        core = c + p * (1 - 2 * c)
+        return (oy * (side // 2) + ox // 2) * CORES + core, (oy * side + ox) * CORES + core
+
+    def root_copy(peer, sem, place, half, src=None, dst=None, recv=None):
+        here = lroot.at[2 * place + half]
+        return pltpu.make_async_remote_copy(
+            src_ref=here if src is None else src, dst_ref=here if dst is None else dst, send_sem=l_send.at[sem],
+            recv_sem=l_recv.at[2 * place + half] if recv is None else recv, device_id={"tensor": peer}, device_id_type=MESH)
+
+    sent = [0, 0, 0, 0]
+
+    def root_send(peer, sem, place, half, **kw):
+        sent[sem] += 1
+        root_copy(peer, sem, place, half, **kw).start()
+
+    def root_wait(place, half):
+        root_copy(twin, 3, place, half).wait_recv()
+
+    own_place, _ = root_block(0, 0)
+    far_place, _ = root_block(0, 1)
+    passing = (y * (side // 2) + ((x - dx + side) % side) // 2) * CORES + c
+
+    def root_start():
+        for half in (0, 1):
+            root_send(helper, 0, own_place, half, src=lr_ref.at[half], dst=relay.at[half], recv=relay_recv.at[half])
+            root_send(up, 1, own_place, half, src=lr_ref.at[half])
+            root_send(down, 2, own_place, 1 - half, src=lr_ref.at[1 - half])
+        for half in (0, 1):
+            root_send(twin, 3, own_place, half, src=lr_ref.at[half])
+
+    def root_relay():
+        for half in (0, 1):
+            root_copy(helper, 0, own_place, half, src=lr_ref.at[half], dst=relay.at[half], recv=relay_recv.at[half]).wait_recv()
+            root_send(helper, 0, passing, half, src=relay.at[half])
+
+    def root_far():
+        for half in (0, 1):
+            root_wait(far_place, half)
+            root_send(up, 1, far_place, half)
+            root_send(down, 2, far_place, half)
+            root_send(twin, 3, far_place, half)
+
+    def root_round(r):
+        q, stage = r // 3, r % 3
+        if stage < 2:
+            up_half = stage if q == 0 else stage
+            down_half = 1 - stage if q == 0 else stage
+            below, above = root_block(side - 1, q)[0], root_block(1, q)[0]
+        else:
+            up_half, down_half = 0, 1
+            below = above = root_block(2, q)[0]
+        root_wait(below, up_half)
+        if stage < 2 and up_half == 0:
+            root_send(up, 1, below, 0)
+        root_send(twin, 3, below, up_half)
+        root_wait(above, down_half)
+        if stage < 2 and down_half == 1:
+            root_send(down, 2, above, 1)
+        root_send(twin, 3, above, down_half)
+
+    steps(grad, gbuf, load_sem, GRAD_ROUND_STEP, [(ROOT_START_STEP, root_start)], grad_work)
+
+    x_copy = pltpu.make_async_remote_copy(
+        src_ref=xx.at[0], dst_ref=xx.at[1], send_sem=x_send.at[0], recv_sem=x_recv.at[0], device_id={"tensor": helper}, device_id_type=MESH)
+    xx[0] = acc[:, :cols].astype(jnp.bfloat16)
+    root_relay()
+    x_copy.start()
+    root_round(0)
 
     def left_step(t, carry):
         at = pl.ds(pl.multiple_of(t * lrows, lrows), lrows)
         lo_ref[:, at] = EMA_DECAY * lo_ref[:, at] + (1.0 - EMA_DECAY) * acc[at, cols:].T
         return carry
     lax.fori_loop(0, rows // lrows, left_step, 0)
-    left_store = pltpu.make_async_copy(lo_ref, lo_out, out_sem.at[1])
-    left_store.start()
-
-    def root_work(k, slot, b):
-        left = lbuf[slot].reshape(lrows, rows)
-        at = pl.ds(pl.multiple_of(b * lrows, lrows), lrows)
-        do_ref[at, :] = jnp.dot(left, xbf[...], preferred_element_type=jnp.float32)
-        pltpu.make_async_copy(do_ref.at[at], do_out.at[at], out_sem.at[2]).start()
-
-    steps(root, lbuf, load_sem, ROOT_ROUND_STEP, [], root_work)
+
+    def at_step(i):
+        e, p = i // 2, i % 2
+        dy = lax.shift_right_logical(ROOT_Y, 2 * e) & 3
+        q = lax.shift_right_logical(ROOT_X, 2 * e) & 3
+        return root_block(dy, q, p)
+
+    def twin_wait(i, place):
+        @pl.when(i % 2 == 1)
+        def _():
+            root_wait(place, 0)
+            root_wait(place, 1)
+
+    def product(place, which):
+        left = lroot[pl.ds(2 * place, 2)].reshape(lrows, rows)
+        return jnp.dot(left, xx[which], preferred_element_type=jnp.float32)
+
+    def rows_of(device):
+        return pl.ds(pl.multiple_of(device * lrows, lrows), lrows)
+
+    def own_rows(i):
+        place, device = at_step(i)
+        do_ref[rows_of(device), :] = product(place, 0)
+
+    def lent_copy(place, device):
+        return pltpu.make_async_remote_copy(
+            src_ref=lent.at[place], dst_ref=do_ref.at[rows_of(device)], send_sem=d_send.at[0], recv_sem=d_recv.at[place],
+            device_id={"tensor": client}, device_id_type=MESH)
+
+    def lent_rows(i):
+        place, device = at_step(i)
+        lent[place] = product(place, 1)
+        lent_copy(place, device).start()
+
+    def loop(lo, hi, body):
+        def step(i, carry):
+            body(i)
+            return carry
+        lax.fori_loop(lo, hi, step, 0)
+
+    def first_own(i):
+        @pl.when(i == 2)
+        def _():
+            root_far()
+            root_round(1)
+
+        @pl.when(i == 8)
+        def _():
+            root_round(2)
+        twin_wait(i, at_step(i)[0])
+        own_rows(i)
+
+    loop(0, 10, first_own)
+    root_round(3)
+    x_copy.wait_recv()
+    loop(0, 10, lent_rows)
+    root_round(4)
+
+    def both(i):
+        twin_wait(i, at_step(i)[0])
+        lent_rows(i)
+        own_rows(i)
+    loop(10, 14, both)
+    root_round(5)
+
+    def last_lent(i):
+        twin_wait(i, at_step(i)[0])
+        lent_rows(i)
+    loop(14, 16, last_lent)
+    loop(14, 16, own_rows)
+
     grad.drain()
-    root.drain()
-    pltpu.make_async_copy(ro_ref, ro_out, out_sem.at[0]).wait()
-    left_store.wait()
-    pltpu.make_async_copy(do_ref, do_out, out_sem.at[2]).wait()
+    for sem, count in enumerate(sent):
+        whole = lroot.at[pl.ds(0, count)]
+        pltpu.make_async_copy(whole, whole, l_send.at[sem]).wait()
+    x_copy.wait_send()
+    pltpu.make_async_copy(lent, lent, d_send.at[0]).wait()
+
+    def lent_wait(i, carry):
+        lent_copy(i, 0).wait_recv()
+        return carry
+    lax.fori_loop(0, half_count // 2, lent_wait, 0)
+
+
+def store_kernel(*refs):
+    count = (len(refs) - 1) // 2
+    sems = refs[-1]
+    pieces = 4
+    for i in range(count):
+        src, dst = refs[i], refs[count + i]
+        step = src.shape[0] // pieces
+        for j in range(pieces):
+            part = pl.ds(j * step, step)
+            pltpu.make_async_copy(src.at[part], dst.at[part], sems.at[i]).start()
+    for i in range(count):
+        pltpu.make_async_copy(refs[i], refs[count + i], sems.at[i]).wait()
 
 
 def solution(mesh):
@@ -253,41 +413,55 @@
     def local_step(g, l, r, lr, rr):
         rows, cols = g.shape
         lrows = l.shape[0]
+        kept = n // 2
         hbm = pl.BlockSpec(memory_space=pltpu.HBM)
-        left_new, right_new, direction, _, _ = pl.pallas_call(
+        vmem = pl.BlockSpec(memory_space=pltpu.VMEM)
+        operands = [g.reshape(2, rows // 2, cols), l, r, lr.reshape(2, lrows // 2, rows), rr]
+        left_new, right_new, direction, _ = pl.pallas_call(
             functools.partial(kernel, n, side),
             name="shampoo",
             out_shape=[
-                jax.ShapeDtypeStruct(l.shape, jnp.float32),
-                jax.ShapeDtypeStruct(r.shape, jnp.float32),
-                jax.ShapeDtypeStruct(g.shape, jnp.float32),
-                jax.ShapeDtypeStruct((2 * n, rows // 2, cols), jnp.bfloat16),
-                jax.ShapeDtypeStruct((2 * n, lrows // 2, rows), jnp.bfloat16),
-            ],
-            in_specs=[hbm] * 5,
-            out_specs=[hbm] * 5,
-            scratch_shapes=[
                 pltpu.VMEM(l.shape, jnp.float32),
                 pltpu.VMEM(r.shape, jnp.float32),
                 pltpu.VMEM(g.shape, jnp.float32),
+                pltpu.HBM((2 * n, rows // 2, cols), jnp.bfloat16),
+            ],
+            in_specs=[hbm] * 5,
+            out_specs=[vmem, vmem, vmem, hbm],
+            scratch_shapes=[
                 pltpu.VMEM(rr.shape, jnp.bfloat16),
                 pltpu.VMEM((cols, rows), jnp.bfloat16),
                 pltpu.VMEM((rows, cols + lrows), jnp.float32),
                 pltpu.VMEM((2, 2, rows // 2, cols), jnp.bfloat16),
-                pltpu.VMEM((2, 2, lrows // 2, rows), jnp.bfloat16),
                 pltpu.VMEM((cols + lrows, cols), jnp.bfloat16),
-                pltpu.VMEM((rows, cols), jnp.bfloat16),
-                pltpu.SemaphoreType.DMA((2 * n,)),
+                pltpu.VMEM((2, rows, cols), jnp.bfloat16),
+                pltpu.VMEM((2 * kept, lrows // 2, rows), jnp.bfloat16),
+                pltpu.VMEM((2, lrows // 2, rows), jnp.bfloat16),
+                pltpu.VMEM((kept, lrows, cols), jnp.float32),
                 pltpu.SemaphoreType.DMA((2 * n,)),
                 pltpu.SemaphoreType.DMA((5,)),
-                pltpu.SemaphoreType.DMA((5,)),
                 pltpu.SemaphoreType.DMA((2,)),
-                pltpu.SemaphoreType.DMA((3,)),
-                pltpu.SemaphoreType.DMA((3,)),
+                pltpu.SemaphoreType.DMA((4,)),
+                pltpu.SemaphoreType.DMA((2 * kept,)),
+                pltpu.SemaphoreType.DMA((2,)),
+                pltpu.SemaphoreType.DMA((1,)),
+                pltpu.SemaphoreType.DMA((kept,)),
+                pltpu.SemaphoreType.DMA((4,)),
+                pltpu.SemaphoreType.DMA((1,)),
+                pltpu.SemaphoreType.DMA((1,)),
             ],
-            compiler_params=pltpu.CompilerParams(collective_id=0, has_side_effects=True, vmem_limit_bytes=62 * 2**20),
+            compiler_params=pltpu.CompilerParams(collective_id=0, has_side_effects=True, vmem_limit_bytes=48 * 2**20),
             cost_estimate=pl.CostEstimate(flops=2 * rows * cols * (2 * n * cols + 2 * rows), bytes_accessed=2 * n * rows * cols * 3, transcendentals=0),
-        )(g.reshape(2, rows // 2, cols), l, r, lr.reshape(2, lrows // 2, rows), rr)
-        return left_new, right_new, direction
+        )(*[pltpu.with_memory_space_constraint(v, pltpu.HBM) for v in operands])
+        results = [left_new, right_new, direction]
+        return pl.pallas_call(
+            store_kernel,
+            name="store",
+            out_shape=[jax.ShapeDtypeStruct(v.shape, v.dtype) for v in results],
+            in_specs=[vmem] * 3,
+            out_specs=[hbm] * 3,
+            scratch_shapes=[pltpu.SemaphoreType.DMA((3,))],
+            compiler_params=pltpu.CompilerParams(vmem_limit_bytes=1 * 2**20),
+        )(*results)
 
     return jax.shard_map(local_step, mesh=mesh, in_specs=(col_spec, row_spec, row_spec, row_spec, row_spec), out_specs=(row_spec, row_spec, col_spec), check_vma=False)

time: 286 us -> 263 us (0.920)
  local copies, waits for them, and re-layouts: 13 us -> 0 us
  Pallas kernels: 271 us -> 262 us
    pallas_call x1, Pallas kernels: 271 us -> 257 us  [local_step(): pl.pallas_call(functools.partial(kernel, n, side), name='shampoo', out_sh...]
    unnamed x5 -> x0, local copies, waits for them, and re-layouts: 13 us -> none
    pallas_call x0 -> x1, Pallas kernels: none -> 5.22 us  [local_step(): pl.pallas_call(store_kernel, name='store', out_shape=[jax.ShapeDtypeStruc...]
where the time goes in v3:
time: 263 us; the launch traced here: 262 us
  Pallas kernels  262 us (100%)
    pallas_call x1, Pallas kernels, local_step(): pl.pallas_call(functools.partial(kernel, n, side), name='shampoo', out_sh...  257 us

profile of v3, /device:TPU:97, one launch (start us, length us, event | category | flops | bytes accessed | tf_op | source)
XLA Modules:
  0.0 262.5 jit_solution(13653035465412535946)
XLA Ops:
  0.6 256.6 %shampoo.1 = (f32[128,4096]{1,0:T(8,128)S(1)}, f32[256,8192]{1,0:T(8,128)S(1)}, f32[4096,256]{1,0:T(8,128)S(1)}, bf16[64,2048,256]{2,1,0:T(8,128)(2,1)}) custom-call(bf16[2,2048,256]{2,1,0:T(8,128)(2,1)} %bitcast.2, f32[128,4096]{1,0:T(8,128)} %l_ref.1, f32[256,8192]{1,0:T(8,128)} %r_ref.1, bf16[2,64,4096]{2,1,0:T(8,128)(2,1)} %bitcast.3, ...), custom_call_target="tpu_custom_call" | custom-call | flops 51539607552 | bytes 201326592 | tf_op jit(solution)/shard_map/shampoo/pallas_call | solution.py:420
  257.2 5.2 %store.1 = (f32[128,4096]{1,0:T(8,128)}, f32[256,8192]{1,0:T(8,128)}, f32[4096,256]{1,0:T(8,128)}) custom-call(f32[128,4096]{1,0:T(8,128)S(1)} %get-tuple-element.6.refs_0_, f32[256,8192]{1,0:T(8,128)S(1)} %get-tuple-element.7.refs_1_, f32[4096,256]{1,0:T(8,128)S(1)} %get-tuple-element.8.refs_2_), custom_call_target="tpu_custom_call" | custom-call | tf_op jit(solution)/shard_map/store/pallas_call | solution.py:457
